TPU v7x, 32 devices: a whole 2x2x4 slice. The times are simulated.
32 devices in a mesh: wide: 16 (over z, y, core), narrow: 2 (over x).
Axes of the slice: x: 2, y: 2, z: 4, core: 2. Of those that a mesh axis runs over, the one named last changes fastest.
Arguments:
- src_field: bfloat16 [2, 16, 65536], P(None, 'narrow', 'wide'), may hold values from -6 to 6
- src_depth: int32 [65536], P(('wide', 'narrow')), may hold values from 0 to 16, as said below
- packed_counts: int32 [4096, 64, 128], P(('wide', 'narrow')), may hold values from 0 to 100664832, as said below
- pair_source: int32 [4096], P(('wide', 'narrow')), may hold values from 0 to 15
- pair_home: int32 [4096], P(('wide', 'narrow')), may hold values from 0 to 1023, as said below
- pair_count: int32 [32], P(('wide', 'narrow')), may hold values from 64 to 128, as said below
Outputs:
- remapped: bfloat16 [2, 16, 131072], P(None, 'narrow', 'wide')
Inputs may be any that keep to these rules, and one draw needn't show every extreme that they name: `src_depth`: depth 0 marks a dry source cell. `packed_counts`: word (p, i, j) holds count (p, i, j) plus 65536 times count (p, i + 64, j); every count lies between 0 and 1536. The target block pair_home[p] is held by wide index pair_home[p] // 64, which differs by at most 2, counted cyclically over the wide axis, from the wide index of the device that holds pair p. Among the 128 pairs of one device at most 51 have target blocks on one wide index, and on some wide index exactly 51 live pairs of that device. A device's pairs from position pair_count[d] on are padding; some device has all 128 live.
All inputs are finite; a program needn't handle non-finite values.
Results may differ from a plain program's by a relative error of at most 0.0054.
Values may be sent and summed in bfloat16 or wider, within the bound.
A program may use at most 64 MiB of HBM per device.

v0:
```python
import jax
import jax.numpy as jnp
from jax import lax
from jax.sharding import PartitionSpec as P

DENOM = 256
REACH = 2
TB_DEV = 64


wet_limit = 0.001


def passed_along(block, axis, distance):
    devices = range(lax.axis_size(axis))
    route = [((i - distance) % len(devices), i) for i in devices]
    return lax.ppermute(block, axis, route)


def unpack_counts(packed_words):
    return jnp.concatenate([packed_words % 65536, packed_words // 65536], axis=-2)


def block_sums(targets, received, block_count):
    owners = jnp.arange(block_count, dtype=jnp.int32)
    select = (targets[:, None] == owners[None, :]).astype(jnp.bfloat16)
    return jnp.einsum("rq,rlcb->lcqb", select, received, preferred_element_type=jnp.float32)


def per_device(src_field, src_depth, packed_counts, pair_source, pair_home, pair_count):
    narrow_size = lax.axis_size("narrow")
    wide_size = lax.axis_size("wide")
    field_vars = src_field.shape[0]
    components = field_vars + 1
    block_cells = packed_counts.shape[2]
    own_cells = src_depth.shape[0]
    own_tiles = own_cells // block_cells
    pair_slots = pair_source.shape[0]
    offset_count = 2 * REACH + 1
    capacity = max(2, 2 * pair_slots // offset_count)
    own_field = lax.all_to_all(src_field, "narrow", split_axis=2, concat_axis=1, tiled=True)
    levels = own_field.shape[1]
    part_levels = levels // narrow_size
    level_ids = jnp.arange(levels, dtype=jnp.int32)
    wet_levels = level_ids[:, None] < src_depth[None, :]
    masked = jnp.where(wet_levels[None, :, :], own_field, jnp.zeros_like(own_field))
    stacked = jnp.concatenate(
        [jnp.transpose(masked, (1, 0, 2)), wet_levels.astype(jnp.bfloat16)[:, None, :]], axis=1
    )
    by_tile = jnp.transpose(stacked.reshape(levels * components, own_tiles, block_cells), (1, 0, 2))
    picked = jnp.take(by_tile, pair_source, axis=0)
    weight = (unpack_counts(packed_counts).astype(jnp.float32) / DENOM).astype(jnp.bfloat16)
    pair_terms = lax.dot_general(
        picked, weight, (((2,), (2,)), ((0,), (0,))), preferred_element_type=jnp.float32
    )
    pair_terms = pair_terms.astype(jnp.bfloat16)
    is_live = jnp.arange(pair_slots, dtype=jnp.int32) < pair_count[0]
    wide_index = lax.axis_index("wide")
    destination = pair_home // TB_DEV
    local_block = pair_home % TB_DEV
    offset_index = (destination - wide_index + REACH + wide_size) % wide_size
    bound_for = (
        (offset_index[:, None] == jnp.arange(offset_count, dtype=jnp.int32)[None, :])
        & is_live[:, None]
    ).astype(jnp.int32)
    before = jnp.cumsum(bound_for, axis=0) - bound_for
    position = jnp.sum(before * bound_for, axis=1)
    slot_index = jnp.where(is_live, offset_index * capacity + position, offset_count * capacity)
    outgoing = (
        jnp.zeros((offset_count * capacity, levels * components, block_cells), jnp.bfloat16)
        .at[slot_index]
        .set(pair_terms, mode="drop")
    )
    targets = (
        jnp.full((offset_count * capacity,), TB_DEV, jnp.int32)
        .at[slot_index]
        .set(local_block, mode="drop")
    )
    outgoing = outgoing.reshape(offset_count, capacity, levels, components, block_cells)
    targets = targets.reshape(offset_count, capacity)
    shift_list = [shift_by for shift_by in range(-REACH, REACH + 1) if shift_by != 0]
    partial_value = block_sums(targets[REACH], outgoing[REACH], TB_DEV)
    for shift_by in shift_list:
        moved_terms, moved_owners = passed_along(
            (outgoing[REACH + shift_by], targets[REACH + shift_by]), "wide", shift_by
        )
        partial_value = partial_value + block_sums(moved_owners, moved_terms, TB_DEV)
    block_totals = lax.psum_scatter(partial_value, "narrow", scatter_dimension=0, tiled=True)
    numerators = block_totals[:, :field_vars]
    wet_total = block_totals[:, field_vars]
    covered = wet_total > wet_limit
    safe_wet = jnp.where(covered, wet_total, jnp.ones_like(wet_total))
    result = jnp.where(covered[:, None], numerators / safe_wet[:, None], jnp.zeros_like(numerators))
    result = jnp.transpose(result, (1, 0, 2, 3)).reshape(
        field_vars, part_levels, TB_DEV * block_cells
    )
    return result.astype(jnp.bfloat16)


def solution(mesh):
    placed = (
        P(None, "narrow", "wide"),
        P(("wide", "narrow")),
        P(("wide", "narrow"), None, None),
        P(("wide", "narrow")),
        P(("wide", "narrow")),
        P(("wide", "narrow")),
    )
    return jax.shard_map(
        per_device, mesh=mesh, in_specs=placed, out_specs=P(None, "narrow", "wide"), check_vma=False
    )
```

profile of v0, /device:TPU:0, one launch (start us, length us, event | category | flops | bytes accessed | tf_op | source)
XLA Modules:
  0.0 141.5 jit_solution(15521793403621437424)
XLA Ops:
  6.5 4.4 %copy.29 = bf16[2,8,4096]{1,0,2:T(2,128)(2,1)S(1)} copy(bf16[2,8,4096]{2,1,0:T(8,128)(2,1)} %param.6) | data formatting | bytes 262144 | tf_op args[0]
  10.9 2.8 %reshape.126 = bf16[2,2,16384]{2,1,0:T(2,128)(2,1)} reshape(bf16[4096,2,8]{2,1,0:T(2,128)(2,1)S(1)} %bitcast.60) | data formatting | bytes 262144
  13.8 4.2 %all-to-all-start = ((bf16[2,2,16384]{2,1,0:T(2,128)(2,1)}), bf16[2,2,16384]{2,1,0:T(2,128)(2,1)S(1)}, u32[]{:S(2)}, u32[]{:S(2)}) async-start(bf16[2,2,16384]{2,1,0:T(2,128)(2,1)} %reshape.126), calls=%async_computation | async-start | bytes 262144 | tf_op jit(solution)/shard_map/all_to_all | solution.py:41
  18.0 0.0 reduce-scatter.2.cloned.1.call-start
  18.0 0.0 copy-done.3
  18.0 0.1 compare_convert_fusion
  18.2 0.0 copy-done.5
  18.9 0.1 fusion.29
  19.0 0.2 reduce_window_sum.11
  19.2 0.2 select_reduce_fusion
  19.4 7.1 %add_select_fusion.1 = (s32[128,64,128]{2,1,0:T(8,128)}, s32[128,64,128]{2,1,0:T(8,128)}) fusion(s32[128,64,128]{2,1,0:T(8,128)} %param.8), kind=kLoop, calls=%fused_computation.8 | loop fusion | flops 19922944 | bytes 12582912 | tf_op jit(solution)/shard_map/jit(remainder)/select_n | solution.py:21
  26.5 0.0 all-to-all-done
  26.5 2.5 %reshape.127 = bf16[4096,2,8]{2,1,0:T(2,128)(2,1)S(1)} reshape(bf16[2,2,16384]{2,1,0:T(2,128)(2,1)S(1)} %all-to-all-done) | data formatting | bytes 262144
  28.9 1.4 copy.30
  30.3 0.2 fusion.27
  30.6 0.3 pad_maximum_fusion
  30.9 0.2 reshape.91
  31.1 0.1 copy.62
  31.1 0.9 gather_fusion
  32.0 7.7 %fusion.7 = bf16[128,48,128]{2,1,0:T(8,128)(2,1)} fusion(s32[128,64,128]{2,1,0:T(8,128)} %get-tuple-element.6, s32[128,64,128]{2,1,0:T(8,128)} %get-tuple-element.5, bf16[128,48,128]{2,1,0:T(8,128)(2,1)S(1)} %gather_fusion, pred[128]{0:T(512)(128)(4,1)S(1)} %compare_and_fusion), kind=kOutput, calls=%fused_computation.16 | convolution fusion | flops 211288064 | bytes 11534464 | tf_op jit(solution)/shard_map/dot_general | solution.py:53
  39.7 0.4 broadcast_in_dim.71
  40.2 11.7 %scatter_fusion = bf16[255,48,128]{2,1,0:T(8,128)(2,1)S(1)} fusion(bf16[255,48,128]{2,1,0:T(8,128)(2,1)S(1)} %broadcast_in_dim.71, s32[128]{0:T(128)S(1)} %compare_select_fusion.2, bf16[128,48,128]{2,1,0:T(8,128)(2,1)} %fusion.7), kind=kCustom, calls=%fused_computation.1 | custom fusion | bytes 4719104 | tf_op jit(solution)/shard_map/scatter | solution.py:72
  51.9 1.7 %fusion.52 = (bf16[51,48,128]{2,1,0:T(8,128)(2,1)}, bf16[51,48,128]{2,1,0:T(8,128)(2,1)}, bf16[51,48,128]{2,1,0:T(8,128)(2,1)S(1)}, bf16[51,48,128]{2,1,0:T(8,128)(2,1)}, bf16[51,48,128]{2,1,0:T(8,128)(2,1)}) fusion(bf16[255,48,128]{2,1,0:T(8,128)(2,1)S(1)} %scatter_fusion), kind=kLoop, calls=%fused_computation.81 | loop fusion | bytes 6266880 | tf_op jit(solution)/shard_map/slice | solution.py:85
  53.6 0.2 copy.36
  53.8 0.1 copy.37
  53.9 4.8 %collective-permute-start.2 = (bf16[51,16,3,128]{3,1,2,0:T(8,128)(2,1)S(1)}, bf16[51,16,3,128]{3,1,2,0:T(8,128)(2,1)S(1)}, u32[]{:S(2)}, u32[]{:S(2)}) collective-permute-start(bf16[51,16,3,128]{3,1,2,0:T(8,128)(2,1)S(1)} %copy.37), channel_id=1, source_target_pairs={{2,0},{4,2},{6,4},{8,6},{10,8},{12,10},{14,12},{16,14},{18,16},{20... | collective-permute-start | bytes 1880072 | tf_op jit(solution)/shard_map/ppermute | solution.py:17
  58.7 1.0 scatter_custom_fusion.1
  59.6 1.2 copy.33
  60.9 0.1 copy.34
  61.0 0.0 copy-start
  61.0 0.7 collective-permute-start
  61.7 0.1 fusion.53
  61.8 0.3 collective-permute-start.3
  62.1 1.4 collective-permute-start.1
  63.5 0.2 copy.39
  63.7 0.1 copy.40
  63.8 0.2 collective-permute-start.4
  64.0 0.2 copy.32
  64.2 0.5 fusion.31
  64.7 0.0 copy-done
  64.7 0.2 copy.42
  64.9 0.1 copy.43
  65.0 15.0 %collective-permute-done.3 = s32[51]{0:T(128)S(1)} collective-permute-done((s32[51]{0:T(128)S(1)}, s32[51]{0:T(128)S(1)}, u32[]{:S(2)}, u32[]{:S(2)}) %collective-permute-start.3) | collective-permute-done | bytes 236 | tf_op jit(solution)/shard_map/ppermute | solution.py:17
  79.9 4.8 %collective-permute-start.5 = (s32[51]{0:T(128)S(1)}, s32[51]{0:T(128)S(1)}, u32[]{:S(2)}, u32[]{:S(2)}) collective-permute-start(s32[51]{0:T(128)S(1)} %get-tuple-element.13), channel_id=1, source_target_pairs={{30,0},{0,2},{2,4},{4,6},{6,8},{8,10},{10,12},{12,14},{14,16},{16,... | collective-permute-start | bytes 620 | tf_op jit(solution)/shard_map/ppermute | solution.py:17
  84.7 0.0 collective-permute-done.2
  84.7 0.0 collective-permute-start.6
  84.7 0.5 fusion.19
  85.2 0.0 collective-permute-done.1
  85.2 3.1 %collective-permute-start.7 = (s32[51]{0:T(128)S(1)}, s32[51]{0:T(128)S(1)}, u32[]{:S(2)}, u32[]{:S(2)}) collective-permute-start(s32[51]{0:T(128)S(1)} %get-tuple-element.12), channel_id=1, source_target_pairs={{28,0},{30,2},{0,4},{2,6},{4,8},{6,10},{8,12},{10,14},{12,16},{14,... | collective-permute-start | bytes 620 | tf_op jit(solution)/shard_map/ppermute | solution.py:17
  88.3 0.0 collective-permute-done
  88.3 0.5 fusion.21
  88.8 0.0 collective-permute-done.5
  88.8 0.0 collective-permute-done.4
  88.8 0.5 fusion.17
  89.3 14.2 %collective-permute-done.7 = s32[51]{0:T(128)S(1)} collective-permute-done((s32[51]{0:T(128)S(1)}, s32[51]{0:T(128)S(1)}, u32[]{:S(2)}, u32[]{:S(2)}) %collective-permute-start.7) | collective-permute-done | bytes 236 | tf_op jit(solution)/shard_map/ppermute | solution.py:17
  103.5 0.0 collective-permute-done.6
  103.5 1.8 %add_bitcast_fusion = f32[16,3,64,128]{3,2,1,0:T(8,128)} fusion(f32[16,3,128,64]{2,3,1,0:T(8,128)S(1)} %fusion.17, f32[16,3,128,64]{2,3,1,0:T(8,128)S(1)} %fusion.19, f32[16,3,128,64]{2,3,1,0:T(8,128)S(1)} %fusion.31, f32[16,3,128,64]{2,3,1,0:T(8,128)S(1)} %fusion.21, bf16[51,16,3,128]{3,1,2,0:T(8,128)(2,1)S(1)} %collective-permute-done.6, ...), kind=kOutput, calls=%fused_computation.17 | convolution fusion | flops 41684160 | bytes 8491212 | tf_op jit(solution)/shard_map/rq,rlcb->lcqb/dot_general | solution.py:27
  105.4 0.0 reduce-scatter.2.cloned.1.call-update
  105.4 25.2 %reduce-scatter.2.cloned.1.call-done = f32[8,3,64,128]{3,2,1,0:T(8,128)} async-done(((f32[16,3,64,128]{3,2,1,0:T(8,128)}), f32[8,3,64,128]{3,2,1,0:T(8,128)}) %reduce-scatter.2.cloned.1.call-update) | async-done | bytes 786448 | tf_op jit(solution)/shard_map/reduce_scatter | solution.py:88
  130.6 1.0 fusion.25
  131.6 1.0 compare_bitcast_fusion
  132.6 1.1 fusion.26
  133.8 0.1 convert_element_type.43
  133.8 0.9 copy.45
  (15 shorter events, 0.1 us)
Async XLA Ops:
  6.5 11.5 %copy-start.3 = (s32[2048]{0:T(1024)S(1)}, s32[2048]{0:T(1024)}, u32[]{:S(2)}) copy-start(s32[2048]{0:T(1024)} %param.7) | copy-start | bytes 24580
  6.5 11.6 %copy-start.5 = (s32[128]{0:T(128)S(1)}, s32[128]{0:T(128)}, u32[]{:S(2)}) copy-start(s32[128]{0:T(128)} %param.9) | copy-start | bytes 1540
  6.5 12.3 %copy-start.4 = (s32[128]{0:T(128)S(1)}, s32[128]{0:T(128)}, u32[]{:S(2)}) copy-start(s32[128]{0:T(128)} %param.10) | copy-start | bytes 1540
  13.8 12.7 %all-to-all-start = ((bf16[2,2,16384]{2,1,0:T(2,128)(2,1)}), bf16[2,2,16384]{2,1,0:T(2,128)(2,1)S(1)}, u32[]{:S(2)}, u32[]{:S(2)}) async-start(bf16[2,2,16384]{2,1,0:T(2,128)(2,1)} %reshape.126), calls=%async_computation | async-start | bytes 262144 | tf_op jit(solution)/shard_map/all_to_all | solution.py:41
  18.0 112.6 %reduce-scatter.2.cloned.1.call-start = ((), (), s32[]{:S(2)}) async-start(), calls=%async_computation.2 | async-start | bytes 2359296 | tf_op jit(solution)/shard_map/reduce_scatter | solution.py:88
  53.6 9.9 %copy-start.2 = (bf16[51,48,128]{2,1,0:T(8,128)(2,1)S(1)}, bf16[51,48,128]{2,1,0:T(8,128)(2,1)}, u32[]{:S(2)}) copy-start(bf16[51,48,128]{2,1,0:T(8,128)(2,1)} %get-tuple-element.8) | copy-start | bytes 1880068
  53.8 10.2 %copy-start.1 = (bf16[51,48,128]{2,1,0:T(8,128)(2,1)S(1)}, bf16[51,48,128]{2,1,0:T(8,128)(2,1)}, u32[]{:S(2)}) copy-start(bf16[51,48,128]{2,1,0:T(8,128)(2,1)} %get-tuple-element.11) | copy-start | bytes 1880068
  53.9 30.8 %collective-permute-start.2 = (bf16[51,16,3,128]{3,1,2,0:T(8,128)(2,1)S(1)}, bf16[51,16,3,128]{3,1,2,0:T(8,128)(2,1)S(1)}, u32[]{:S(2)}, u32[]{:S(2)}) collective-permute-start(bf16[51,16,3,128]{3,1,2,0:T(8,128)(2,1)S(1)} %copy.37), channel_id=1, source_target_pairs={{2,0},{4,2},{6,4},{8,6},{10,8},{12,10},{14,12},{16,14},{18,16},{20... | collective-permute-start | bytes 1880072 | tf_op jit(solution)/shard_map/ppermute | solution.py:17
  61.0 3.7 %copy-start = (bf16[51,48,128]{2,1,0:T(8,128)(2,1)S(1)}, bf16[51,48,128]{2,1,0:T(8,128)(2,1)}, u32[]{:S(2)}) copy-start(bf16[51,48,128]{2,1,0:T(8,128)(2,1)} %get-tuple-element.7) | copy-start | bytes 1880068
  61.0 27.3 %collective-permute-start = (bf16[51,16,3,128]{3,1,2,0:T(8,128)(2,1)S(1)}, bf16[51,16,3,128]{3,1,2,0:T(8,128)(2,1)S(1)}, u32[]{:S(2)}, u32[]{:S(2)}) collective-permute-start(bf16[51,16,3,128]{3,1,2,0:T(8,128)(2,1)S(1)} %copy.34), channel_id=1, source_target_pairs={{4,0},{6,2},{8,4},{10,6},{12,8},{14,10},{16,12},{18,14},{20,16},{2... | collective-permute-start | bytes 1880072 | tf_op jit(solution)/shard_map/ppermute | solution.py:17
  61.8 18.1 %collective-permute-start.3 = (s32[51]{0:T(128)S(1)}, s32[51]{0:T(128)S(1)}, u32[]{:S(2)}, u32[]{:S(2)}) collective-permute-start(s32[51]{0:T(128)S(1)} %get-tuple-element.14), channel_id=1, source_target_pairs={{2,0},{4,2},{6,4},{8,6},{10,8},{12,10},{14,12},{16,14},{18,16},{20... | collective-permute-start | bytes 620 | tf_op jit(solution)/shard_map/ppermute | solution.py:17
  62.1 23.1 %collective-permute-start.1 = (s32[51]{0:T(128)S(1)}, s32[51]{0:T(128)S(1)}, u32[]{:S(2)}, u32[]{:S(2)}) collective-permute-start(s32[51]{0:T(128)S(1)} %get-tuple-element.15), channel_id=1, source_target_pairs={{4,0},{6,2},{8,4},{10,6},{12,8},{14,10},{16,12},{18,14},{20,16},{2... | collective-permute-start | bytes 620 | tf_op jit(solution)/shard_map/ppermute | solution.py:17
  63.8 25.1 %collective-permute-start.4 = (bf16[51,16,3,128]{3,1,2,0:T(8,128)(2,1)S(1)}, bf16[51,16,3,128]{3,1,2,0:T(8,128)(2,1)S(1)}, u32[]{:S(2)}, u32[]{:S(2)}) collective-permute-start(bf16[51,16,3,128]{3,1,2,0:T(8,128)(2,1)S(1)} %copy.40), channel_id=1, source_target_pairs={{30,0},{0,2},{2,4},{4,6},{6,8},{8,10},{10,12},{12,14},{14,16},{16,... | collective-permute-start | bytes 1880072 | tf_op jit(solution)/shard_map/ppermute | solution.py:17
  79.9 8.9 %collective-permute-start.5 = (s32[51]{0:T(128)S(1)}, s32[51]{0:T(128)S(1)}, u32[]{:S(2)}, u32[]{:S(2)}) collective-permute-start(s32[51]{0:T(128)S(1)} %get-tuple-element.13), channel_id=1, source_target_pairs={{30,0},{0,2},{2,4},{4,6},{6,8},{8,10},{10,12},{12,14},{14,16},{16,... | collective-permute-start | bytes 620 | tf_op jit(solution)/shard_map/ppermute | solution.py:17
  84.7 18.8 %collective-permute-start.6 = (bf16[51,16,3,128]{3,1,2,0:T(8,128)(2,1)S(1)}, bf16[51,16,3,128]{3,1,2,0:T(8,128)(2,1)S(1)}, u32[]{:S(2)}, u32[]{:S(2)}) collective-permute-start(bf16[51,16,3,128]{3,1,2,0:T(8,128)(2,1)S(1)} %copy.43), channel_id=1, source_target_pairs={{28,0},{30,2},{0,4},{2,6},{4,8},{6,10},{8,12},{10,14},{12,16},{14,... | collective-permute-start | bytes 1880072 | tf_op jit(solution)/shard_map/ppermute | solution.py:17
  85.2 18.3 %collective-permute-start.7 = (s32[51]{0:T(128)S(1)}, s32[51]{0:T(128)S(1)}, u32[]{:S(2)}, u32[]{:S(2)}) collective-permute-start(s32[51]{0:T(128)S(1)} %get-tuple-element.12), channel_id=1, source_target_pairs={{28,0},{30,2},{0,4},{2,6},{4,8},{6,10},{8,12},{10,14},{12,16},{14,... | collective-permute-start | bytes 620 | tf_op jit(solution)/shard_map/ppermute | solution.py:17
Sparse Core Ops, SparseCore 0:
  105.5 25.0 reduce-scatter.1
where the time goes:
time: 142 us
  waiting for transfers between devices  54.4 us (38%)
  local copies, waits for them, and re-layouts  30.3 us (21%)
  starting transfers between devices  19.5 us (14%)
  between operations  14.4 us (10%)
  matrix products  11.5 us (8%)
  other arithmetic  11.4 us (8%)
    ppermute x8, waiting for transfers between devices, passed_along(): return lax.ppermute(block, axis, route)  29.2 us
    reduce_scatter x1, waiting for transfers between devices, per_device(): lax.psum_scatter(partial_value, 'narrow', scatter_dimension=0, tiled=True)  25.2 us
    ppermute x8, starting transfers between devices, passed_along(): return lax.ppermute(block, axis, route)  15.3 us
    scatter x1, local copies, waits for them, and re-layouts, per_device(): outgoing = jnp.zeros((offset_count * capacity, levels * components, block...  11.7 us
    unnamed x15, local copies, waits for them, and re-layouts  9.68 us
    dot_general x1, matrix products, per_device(): lax.dot_general(picked, weight, (((2,), (2,)), ((0,), (0,))), preferred_e...  7.73 us
    select_n x1, other arithmetic, unpack_counts(): packed_words % 65536  7.1 us
    all_to_all x1, starting transfers between devices, per_device(): lax.all_to_all(src_field, 'narrow', split_axis=2, concat_axis=1, tiled=True)  4.23 us
  transfers between devices with their start and end apart: 10, of which 3 were waited for; matrix products, arithmetic and copies ran while one was open for 9% of the time, Pallas kernels for 0%

commit v1 on v0

--- a/solution.py
+++ b/solution.py
@@ -1,6 +1,10 @@
+import functools
+
 import jax
 import jax.numpy as jnp
 from jax import lax
+from jax.experimental import pallas as pl
+from jax.experimental.pallas import tpu as pltpu
 from jax.sharding import PartitionSpec as P
 
 DENOM = 256
@@ -27,7 +31,7 @@
     return jnp.einsum("rq,rlcb->lcqb", select, received, preferred_element_type=jnp.float32)
 
 
-def per_device(src_field, src_depth, packed_counts, pair_source, pair_home, pair_count):
+def by_collectives(src_field, src_depth, packed_counts, pair_source, pair_home, pair_count):
     narrow_size = lax.axis_size("narrow")
     wide_size = lax.axis_size("wide")
     field_vars = src_field.shape[0]
@@ -97,6 +101,309 @@
     return result.astype(jnp.bfloat16)
 
 
+SELF, MATE, RELAY, AHEAD, BEHIND = range(5)
+PARTS = 4
+LOADS = 8
+UNROLL = 4
+
+
+def remap_kernel(
+    sizes,
+    field_ref,
+    depth_ref,
+    source_ref,
+    home_ref,
+    packed_ref,
+    out_ref,
+    field_in,
+    home_in,
+    words,
+    weight,
+    stacked,
+    terms,
+    cross_out,
+    cross_in,
+    own_terms,
+    self_sum,
+    sums_out,
+    mate_in,
+    ahead_in,
+    behind_in,
+    load_sems,
+    entry_sems,
+    cross_sems,
+    mate_sems,
+    ahead_sems,
+    behind_sems,
+):
+    wide_size, fields, levels, tiles, cells, pairs = sizes
+    rows = (fields + 1) * levels
+    part_levels = levels // PARTS
+    part_rows = rows // PARTS
+    w = lax.axis_index("wide")
+    n = lax.axis_index("narrow")
+    other = 1 - n
+    sign = 1 - 2 * lax.rem(w, 2)
+    mate = w + sign
+    ahead = lax.rem(w + 2 * sign + wide_size, wide_size)
+    behind = lax.rem(w - 2 * sign + wide_size, wide_size)
+
+    per_load = pairs // LOADS
+    loads = []
+    for i in range(LOADS):
+        span = pl.ds(i * per_load, per_load)
+        load = pltpu.make_async_copy(packed_ref.at[span], words.at[span], load_sems.at[i])
+        load.start()
+        loads.append(load)
+
+    def remote(src, dst, sems, index, place):
+        return pltpu.make_async_remote_copy(
+            src_ref=src,
+            dst_ref=dst,
+            send_sem=sems.at[0, index],
+            recv_sem=sems.at[1, index],
+            device_id=place,
+            device_id_type=pl.DeviceIdType.MESH,
+        )
+
+    barrier = pltpu.get_barrier_semaphore()
+    for place in ((w, other), (mate, n), (ahead, n), (behind, n)):
+        pl.semaphore_signal(
+            barrier, inc=1, device_id=place, device_id_type=pl.DeviceIdType.MESH
+        )
+    pl.semaphore_wait(barrier, 4)
+
+    own_cells = tiles * cells
+    entry = [
+        remote(
+            field_ref.at[:, :, pl.ds(pl.multiple_of(other * own_cells, own_cells), own_cells)],
+            field_in,
+            entry_sems,
+            0,
+            (w, other),
+        ),
+        remote(home_ref, home_in, entry_sems, 1, (w, other)),
+    ]
+    for copy in entry:
+        copy.start()
+
+    level_ids = lax.broadcasted_iota(jnp.int32, (levels, cells), 0)
+
+    def stack(side, group, read):
+        for tile in range(tiles):
+            wet = level_ids + group * levels < depth_ref[pl.ds(tile, 1), :]
+            for k in range(fields):
+                value = read(k, tile).astype(jnp.float32)
+                stacked[side * tiles + tile, pl.ds(k * levels, levels), :] = jnp.where(
+                    wet, value, 0.0
+                )
+            stacked[side * tiles + tile, pl.ds(fields * levels, levels), :] = jnp.where(
+                wet, 1.0, 0.0
+            )
+
+    own_start = n * own_cells
+    stack(
+        0,
+        n,
+        lambda k, tile: field_ref[
+            k, :, pl.ds(pl.multiple_of(own_start + tile * cells, cells), cells)
+        ],
+    )
+
+    half = cells // 2
+    for i in range(LOADS):
+        loads[i].wait()
+
+        def unpack(step, carry):
+            for u in range(UNROLL):
+                p = i * per_load + step * UNROLL + u
+                word = words[p]
+                low = (word & 65535).astype(jnp.float32).astype(jnp.bfloat16)
+                high = (word >> 16).astype(jnp.float32).astype(jnp.bfloat16)
+                weight[p, pl.ds(0, half), :] = low
+                weight[p, pl.ds(half, half), :] = high
+            return carry
+
+        lax.fori_loop(0, per_load // UNROLL, unpack, 0)
+
+    entry[0].wait()
+    stack(1, other, lambda k, tile: field_in[k, :, pl.ds(tile * cells, cells)])
+
+    def multiply(side):
+        def body(step, carry):
+            for u in range(UNROLL):
+                p = step * UNROLL + u
+                values = stacked[side * tiles + source_ref[p]].astype(jnp.bfloat16)
+                term = lax.dot_general(
+                    values, weight[p], (((1,), (1,)), ((), ())),
+                    preferred_element_type=jnp.float32,
+                )
+                terms[pl.ds(p, rows, stride=pairs), :] = term * (1.0 / DENOM)
+            return carry
+
+        lax.fori_loop(0, pairs // UNROLL, body, 0)
+
+    def rounded(part, row):
+        k, level = row // part_levels, part * part_levels + row % part_levels
+        return terms[pl.ds((k * levels + level) * pairs, pairs), :].astype(jnp.bfloat16)
+
+    multiply(1)
+    cross = []
+    for part in range(PARTS):
+        for row in range(part_rows):
+            cross_out[part, row] = rounded(part, row)
+        copy = remote(cross_out.at[part], cross_in.at[part], cross_sems, part, (w, other))
+        copy.start()
+        cross.append(copy)
+
+    multiply(0)
+    for part in range(PARTS):
+        for row in range(part_rows):
+            own_terms[part, row] = rounded(part, row)
+
+    entry[1].wait()
+    slots = lax.broadcasted_iota(jnp.int32, (5 * TB_DEV, pairs), 0)
+    select = jnp.concatenate(
+        [
+            jnp.where(slots == home_ref[...], 1.0, 0.0).astype(jnp.bfloat16),
+            jnp.where(slots == home_in[...], 1.0, 0.0).astype(jnp.bfloat16),
+        ],
+        axis=1,
+    )
+
+    to_mate, to_ahead, to_behind = [], [], []
+
+    def pass_on(part):
+        to_mate[part].wait_recv()
+        for row in range(part_rows):
+            sums_out[part, AHEAD - 1, row] = (
+                sums_out[part, AHEAD - 1, row].astype(jnp.float32)
+                + mate_in[part, RELAY - 1, row].astype(jnp.float32)
+            ).astype(jnp.bfloat16)
+        copy = remote(
+            sums_out.at[part, AHEAD - 1], ahead_in.at[part], ahead_sems, part, (ahead, n)
+        )
+        copy.start()
+        to_ahead.append(copy)
+
+    for part in range(PARTS):
+        cross[part].wait_recv()
+        for row in range(part_rows):
+            pair_values = jnp.concatenate([own_terms[part, row], cross_in[part, row]], axis=0)
+            sums = jnp.dot(select, pair_values, preferred_element_type=jnp.float32)
+            self_sum[part, row] = sums[:TB_DEV]
+            for slot in (MATE, RELAY, AHEAD, BEHIND):
+                sums_out[part, slot - 1, row] = sums[
+                    slot * TB_DEV : (slot + 1) * TB_DEV
+                ].astype(jnp.bfloat16)
+        copy = remote(
+            sums_out.at[part, pl.ds(0, 2)], mate_in.at[part], mate_sems, part, (mate, n)
+        )
+        copy.start()
+        to_mate.append(copy)
+        copy = remote(
+            sums_out.at[part, BEHIND - 1], behind_in.at[part], behind_sems, part, (behind, n)
+        )
+        copy.start()
+        to_behind.append(copy)
+        if part > 0:
+            pass_on(part - 1)
+    pass_on(PARTS - 1)
+
+    for part in range(PARTS):
+        to_behind[part].wait_recv()
+        to_ahead[part].wait_recv()
+
+        def total(row):
+            return (
+                self_sum[part, row]
+                + mate_in[part, MATE - 1, row].astype(jnp.float32)
+                + ahead_in[part, row].astype(jnp.float32)
+                + behind_in[part, row].astype(jnp.float32)
+            )
+
+        for j in range(part_levels):
+            wet_total = total(fields * part_levels + j)
+            covered = wet_total > wet_limit
+            safe_wet = jnp.where(covered, wet_total, 1.0)
+            for k in range(fields):
+                ratio = total(k * part_levels + j) / safe_wet
+                out_ref[k, part * part_levels + j] = jnp.where(covered, ratio, 0.0).astype(
+                    out_ref.dtype
+                )
+    for part in range(PARTS):
+        cross[part].wait_send()
+        to_mate[part].wait_send()
+        to_ahead[part].wait_send()
+        to_behind[part].wait_send()
+
+
+def by_kernel(src_field, src_depth, packed_counts, pair_source, pair_home, pair_count):
+    wide_size = lax.axis_size("wide")
+    fields, levels, _ = src_field.shape
+    pairs, _, cells = packed_counts.shape
+    tiles = src_depth.shape[0] // cells
+    rows = (fields + 1) * levels
+    part_rows = rows // PARTS
+    wide_index = lax.axis_index("wide")
+    sign = 1 - 2 * (wide_index % 2)
+    offset = (pair_home // TB_DEV - wide_index + REACH + wide_size) % wide_size - REACH
+    toward = offset * sign
+    slot = jnp.where(toward > 0, 2 * toward - 1, -2 * toward)
+    is_live = jnp.arange(pairs, dtype=jnp.int32) < pair_count[0]
+    home = jnp.where(is_live, slot * TB_DEV + pair_home % TB_DEV, -1)
+    sizes = (wide_size, fields, levels, tiles, cells, pairs)
+    vmem = pl.BlockSpec(memory_space=pltpu.VMEM)
+    bf16, f32, i32 = jnp.bfloat16, jnp.float32, jnp.int32
+    sums_shape = (PARTS, part_rows, TB_DEV, cells)
+    copies = pltpu.SemaphoreType.DMA((2, PARTS))
+    result = pl.pallas_call(
+        functools.partial(remap_kernel, sizes),
+        out_shape=jax.ShapeDtypeStruct((fields, levels, TB_DEV, cells), bf16),
+        in_specs=[
+            vmem,
+            vmem,
+            pl.BlockSpec(memory_space=pltpu.SMEM),
+            vmem,
+            pl.BlockSpec(memory_space=pl.ANY),
+        ],
+        out_specs=vmem,
+        scratch_shapes=[
+            pltpu.VMEM((fields, levels, tiles * cells), bf16),
+            pltpu.VMEM((1, pairs), i32),
+            pltpu.VMEM((pairs, cells // 2, cells), i32),
+            pltpu.VMEM((pairs, cells, cells), bf16),
+            pltpu.VMEM((2 * tiles, rows, cells), f32),
+            pltpu.VMEM((rows * pairs, cells), f32),
+            pltpu.VMEM((PARTS, part_rows, pairs, cells), bf16),
+            pltpu.VMEM((PARTS, part_rows, pairs, cells), bf16),
+            pltpu.VMEM((PARTS, part_rows, pairs, cells), bf16),
+            pltpu.VMEM(sums_shape, f32),
+            pltpu.VMEM((PARTS, 4) + sums_shape[1:], bf16),
+            pltpu.VMEM((PARTS, 2) + sums_shape[1:], bf16),
+            pltpu.VMEM(sums_shape, bf16),
+            pltpu.VMEM(sums_shape, bf16),
+            pltpu.SemaphoreType.DMA((LOADS,)),
+            pltpu.SemaphoreType.DMA((2, 2)),
+            copies,
+            copies,
+            copies,
+            copies,
+        ],
+        compiler_params=pltpu.CompilerParams(
+            collective_id=0, has_side_effects=True, vmem_limit_bytes=48 * 1024 * 1024
+        ),
+        name="remap",
+    )(
+        src_field,
+        src_depth.reshape(tiles, cells),
+        pair_source,
+        home.reshape(1, pairs),
+        packed_counts,
+    )
+    return result.reshape(fields, levels, TB_DEV * cells)
+
+
 def solution(mesh):
     placed = (
         P(None, "narrow", "wide"),
@@ -106,6 +413,12 @@
         P(("wide", "narrow")),
         P(("wide", "narrow")),
     )
+    paired = mesh.shape["narrow"] == 2 and mesh.shape["wide"] % 2 == 0
+    fits = paired and mesh.shape["wide"] > 2 * REACH and REACH == 2
     return jax.shard_map(
-        per_device, mesh=mesh, in_specs=placed, out_specs=P(None, "narrow", "wide"), check_vma=False
-    )
+        by_kernel if fits else by_collectives,
+        mesh=mesh,
+        in_specs=placed,
+        out_specs=P(None, "narrow", "wide"),
+        check_vma=False,
+    )

time: 142 us -> 48.2 us (0.34)
  waiting for transfers between devices: 54.4 us -> 0 us
  Pallas kernels: 0 us -> 41.4 us
  local copies, waits for them, and re-layouts: 30.3 us -> 5.25 us
  starting transfers between devices: 19.5 us -> 0 us
  between operations: 14.4 us -> 0.67 us
  matrix products: 11.5 us -> 0 us
  other arithmetic: 11.4 us -> 0.68 us
    pallas_call x0 -> x1, Pallas kernels: none -> 41.4 us  [by_kernel(): pl.pallas_call(functools.partial(remap_kernel, sizes), out_shape=jax.Shap...]
    ppermute x8 -> x0, waiting for transfers between devices: 29.2 us -> none  [passed_along(): return lax.ppermute(block, axis, route)]
    reduce_scatter x1 -> x0, waiting for transfers between devices: 25.2 us -> none  [per_device(): lax.psum_scatter(partial_value, 'narrow', scatter_dimension=0, tiled=True)]
    ppermute x8 -> x0, starting transfers between devices: 15.3 us -> none  [passed_along(): return lax.ppermute(block, axis, route)]
    scatter x2 -> x0, local copies, waits for them, and re-layouts: 12.7 us -> none  [the longest x1 11.7 us: per_device(): outgoing = jnp.zeros((offset_count * capacity, levels * components, block...]
    dot_general x6 -> x0, matrix products: 11.5 us -> none  [the longest x1 7.73 us: per_device(): lax.dot_general(picked, weight, (((2,), (2,)), ((0,), (0,))), preferred_e...]
    select_n x4 -> x0, other arithmetic: 7.13 us -> none  [the longest x1 7.1 us: unpack_counts(): packed_words % 65536]
    unnamed x15 -> x8, local copies, waits for them, and re-layouts: 9.68 us -> 4.44 us
  transfers between devices with their start and end apart: 10 -> 0, of which waited for: 3 -> 0; matrix products, arithmetic and copies ran while one was open for 9% -> 0% of each run, Pallas kernels for 0% -> 0%
where the time goes in v1:
time: 48.2 us; the launch traced here: 48 us
  Pallas kernels  41.4 us (86%)
  local copies, waits for them, and re-layouts  5.25 us (11%)
  other arithmetic  0.68 us (1%)
  between operations  0.67 us (1%)
    pallas_call x1, Pallas kernels, by_kernel(): pl.pallas_call(functools.partial(remap_kernel, sizes), out_shape=jax.Shap...  41.4 us
    unnamed x8, local copies, waits for them, and re-layouts  4.44 us

profile of v1, /device:TPU:0, one launch (start us, length us, event | category | flops | bytes accessed | tf_op | source)
XLA Modules:
  0.0 48.0 jit_solution(574281616682393888)
XLA Ops:
  0.7 0.7 %fusion.5.home_ref = s32[1,128]{1,0:T(1,128)S(1)} fusion(s32[128]{0:T(128)} %param.10, s32[]{:T(128)S(6)} %sub.26, s32[]{:T(128)S(6)} %axis_index.15, s32[]{:T(128)} %bitcast.6), kind=kLoop, calls=%fused_computation.15 | loop fusion | flops 5504 | bytes 1036 | tf_op jit(solution)/shard_map/reshape | solution.py:401
  1.3 0.0 copy-start
  1.3 2.2 %copy-done = s32[128,64,128]{2,1,0:T(8,128)S(1)} copy-done((s32[128,64,128]{2,1,0:T(8,128)S(1)}, s32[128,64,128]{2,1,0:T(8,128)}, u32[]{:S(2)}) %copy-start) | copy-done | bytes 4194328
  3.5 0.0 copy-start.1
  3.5 0.9 %copy-done.1 = bf16[2,8,4096]{2,1,0:T(8,128)(2,1)S(1)} copy-done((bf16[2,8,4096]{2,1,0:T(8,128)(2,1)S(1)}, bf16[2,8,4096]{2,1,0:T(8,128)(2,1)}, u32[]{:S(2)}) %copy-start.1) | copy-done | bytes 131096
  4.4 0.0 copy-start.2
  4.4 0.7 %copy-done.2 = s32[2048]{0:T(1024)S(1)} copy-done((s32[2048]{0:T(1024)S(1)}, s32[2048]{0:T(1024)}, u32[]{:S(2)}) %copy-start.2) | copy-done | bytes 8216
  5.1 0.0 copy-start.3
  5.1 0.7 %copy-done.3 = s32[128]{0:T(128)S(1)} copy-done((s32[128]{0:T(128)S(1)}, s32[128]{0:T(128)}, u32[]{:S(2)}) %copy-start.3) | copy-done | bytes 536
  5.8 41.4 %remap.1 = bf16[2,8,64,128]{3,2,1,0:T(8,128)(2,1)S(1)} custom-call(bf16[2,8,4096]{2,1,0:T(8,128)(2,1)S(1)} %copy-done.1, s32[16,128]{1,0:T(8,128)S(1)} %bitcast.7, s32[128]{0:T(128)S(1)} %copy-done.3, s32[1,128]{1,0:T(1,128)S(1)} %fusion.5.home_ref, s32[128,64,128]{2,1,0:T(8,128)S(1)} %copy-done), custom_call_target="tpu_custom_call" | custom-call | tf_op jit(solution)/shard_map/remap/pallas_call | solution.py:360
  47.1 0.8 %reshape.11 = bf16[2,8,8192]{2,1,0:T(8,128)(2,1)} reshape(bf16[2,8,64,128]{3,2,1,0:T(8,128)(2,1)S(1)} %remap.1) | data formatting | bytes 524288 | tf_op jit(solution)/shard_map/reshape | solution.py:404
Async XLA Ops:
  1.3 2.2 %copy-start = (s32[128,64,128]{2,1,0:T(8,128)S(1)}, s32[128,64,128]{2,1,0:T(8,128)}, u32[]{:S(2)}) copy-start(s32[128,64,128]{2,1,0:T(8,128)} %packed_ref.1) | copy-start | bytes 12582916
  3.5 0.9 %copy-start.1 = (bf16[2,8,4096]{2,1,0:T(8,128)(2,1)S(1)}, bf16[2,8,4096]{2,1,0:T(8,128)(2,1)}, u32[]{:S(2)}) copy-start(bf16[2,8,4096]{2,1,0:T(8,128)(2,1)} %field_ref.1) | copy-start | bytes 393220
  4.4 0.7 %copy-start.2 = (s32[2048]{0:T(1024)S(1)}, s32[2048]{0:T(1024)}, u32[]{:S(2)}) copy-start(s32[2048]{0:T(1024)} %param.7) | copy-start | bytes 24580
  5.1 0.7 %copy-start.3 = (s32[128]{0:T(128)S(1)}, s32[128]{0:T(128)}, u32[]{:S(2)}) copy-start(s32[128]{0:T(128)} %source_ref.1) | copy-start | bytes 1540

commit v2 on v1

v2 whole, which is shorter than its diff:
```python
import functools

import jax
import jax.numpy as jnp
from jax import lax
from jax.experimental import pallas as pl
from jax.experimental.pallas import tpu as pltpu
from jax.sharding import PartitionSpec as P

DENOM = 256
REACH = 2
TB_DEV = 64


wet_limit = 0.001


def passed_along(block, axis, distance):
    devices = range(lax.axis_size(axis))
    route = [((i - distance) % len(devices), i) for i in devices]
    return lax.ppermute(block, axis, route)


def unpack_counts(packed_words):
    return jnp.concatenate([packed_words % 65536, packed_words // 65536], axis=-2)


def block_sums(targets, received, block_count):
    owners = jnp.arange(block_count, dtype=jnp.int32)
    select = (targets[:, None] == owners[None, :]).astype(jnp.bfloat16)
    return jnp.einsum("rq,rlcb->lcqb", select, received, preferred_element_type=jnp.float32)


def by_collectives(src_field, src_depth, packed_counts, pair_source, pair_home, pair_count):
    narrow_size = lax.axis_size("narrow")
    wide_size = lax.axis_size("wide")
    field_vars = src_field.shape[0]
    components = field_vars + 1
    block_cells = packed_counts.shape[2]
    own_cells = src_depth.shape[0]
    own_tiles = own_cells // block_cells
    pair_slots = pair_source.shape[0]
    offset_count = 2 * REACH + 1
    capacity = max(2, 2 * pair_slots // offset_count)
    own_field = lax.all_to_all(src_field, "narrow", split_axis=2, concat_axis=1, tiled=True)
    levels = own_field.shape[1]
    part_levels = levels // narrow_size
    level_ids = jnp.arange(levels, dtype=jnp.int32)
    wet_levels = level_ids[:, None] < src_depth[None, :]
    masked = jnp.where(wet_levels[None, :, :], own_field, jnp.zeros_like(own_field))
    stacked = jnp.concatenate(
        [jnp.transpose(masked, (1, 0, 2)), wet_levels.astype(jnp.bfloat16)[:, None, :]], axis=1
    )
    by_tile = jnp.transpose(stacked.reshape(levels * components, own_tiles, block_cells), (1, 0, 2))
    picked = jnp.take(by_tile, pair_source, axis=0)
    weight = (unpack_counts(packed_counts).astype(jnp.float32) / DENOM).astype(jnp.bfloat16)
    pair_terms = lax.dot_general(
        picked, weight, (((2,), (2,)), ((0,), (0,))), preferred_element_type=jnp.float32
    )
    pair_terms = pair_terms.astype(jnp.bfloat16)
    is_live = jnp.arange(pair_slots, dtype=jnp.int32) < pair_count[0]
    wide_index = lax.axis_index("wide")
    destination = pair_home // TB_DEV
    local_block = pair_home % TB_DEV
    offset_index = (destination - wide_index + REACH + wide_size) % wide_size
    bound_for = (
        (offset_index[:, None] == jnp.arange(offset_count, dtype=jnp.int32)[None, :])
        & is_live[:, None]
    ).astype(jnp.int32)
    before = jnp.cumsum(bound_for, axis=0) - bound_for
    position = jnp.sum(before * bound_for, axis=1)
    slot_index = jnp.where(is_live, offset_index * capacity + position, offset_count * capacity)
    outgoing = (
        jnp.zeros((offset_count * capacity, levels * components, block_cells), jnp.bfloat16)
        .at[slot_index]
        .set(pair_terms, mode="drop")
    )
    targets = (
        jnp.full((offset_count * capacity,), TB_DEV, jnp.int32)
        .at[slot_index]
        .set(local_block, mode="drop")
    )
    outgoing = outgoing.reshape(offset_count, capacity, levels, components, block_cells)
    targets = targets.reshape(offset_count, capacity)
    shift_list = [shift_by for shift_by in range(-REACH, REACH + 1) if shift_by != 0]
    partial_value = block_sums(targets[REACH], outgoing[REACH], TB_DEV)
    for shift_by in shift_list:
        moved_terms, moved_owners = passed_along(
            (outgoing[REACH + shift_by], targets[REACH + shift_by]), "wide", shift_by
        )
        partial_value = partial_value + block_sums(moved_owners, moved_terms, TB_DEV)
    block_totals = lax.psum_scatter(partial_value, "narrow", scatter_dimension=0, tiled=True)
    numerators = block_totals[:, :field_vars]
    wet_total = block_totals[:, field_vars]
    covered = wet_total > wet_limit
    safe_wet = jnp.where(covered, wet_total, jnp.ones_like(wet_total))
    result = jnp.where(covered[:, None], numerators / safe_wet[:, None], jnp.zeros_like(numerators))
    result = jnp.transpose(result, (1, 0, 2, 3)).reshape(
        field_vars, part_levels, TB_DEV * block_cells
    )
    return result.astype(jnp.bfloat16)


SELF, MATE, RELAY, AHEAD, BEHIND = range(5)
LOADS = 8
BATCHES = 4
EARLY = 3
UNROLL = 4


def remap_kernel(
    sizes,
    field_hbm,
    depth_hbm,
    packed_hbm,
    source_hbm,
    home_hbm,
    count_hbm,
    out_ref,
    field,
    depth,
    source,
    home,
    count,
    field_in,
    slot_own,
    slot_in,
    words,
    weight,
    stacked,
    terms,
    cross_out,
    cross_in,
    own_terms,
    self_sum,
    sums_out,
    mate_in,
    ahead_in,
    behind_in,
    load_sems,
    small_sems,
    entry_sems,
    early_sems,
    cross_sems,
    mate_sems,
    ahead_sems,
    behind_sems,
):
    wide_size, fields, levels, tiles, cells, pairs = sizes
    components = fields + 1
    rows = components * levels
    w = lax.axis_index("wide")
    n = lax.axis_index("narrow")
    other = 1 - n
    sign = 1 - 2 * lax.rem(w, 2)
    mate = w + sign
    ahead = lax.rem(w + 2 * sign + wide_size, wide_size)
    behind = lax.rem(w - 2 * sign + wide_size, wide_size)

    barrier = pltpu.get_barrier_semaphore()
    for place in ((w, other), (mate, n), (ahead, n), (behind, n)):
        pl.semaphore_signal(
            barrier, inc=1, device_id=place, device_id_type=pl.DeviceIdType.MESH
        )

    small = []
    for i, (src, dst) in enumerate(
        (
            (field_hbm, field),
            (home_hbm, home),
            (count_hbm, count),
            (depth_hbm, depth),
            (source_hbm, source),
        )
    ):
        load = pltpu.make_async_copy(src, dst, small_sems.at[i])
        load.start()
        small.append(load)
    per_load = pairs // LOADS
    loads = []
    for i in range(LOADS):
        span = pl.ds(i * per_load, per_load)
        load = pltpu.make_async_copy(packed_hbm.at[span], words.at[span], load_sems.at[i])
        load.start()
        loads.append(load)

    def remote(src, dst, sems, index, place):
        return pltpu.make_async_remote_copy(
            src_ref=src,
            dst_ref=dst,
            send_sem=sems.at[(0,) + index],
            recv_sem=sems.at[(1,) + index],
            device_id=place,
            device_id_type=pl.DeviceIdType.MESH,
        )

    small[0].wait()
    small[1].wait()
    small[2].wait()
    wide_home = lax.div(home[...], TB_DEV)
    offset = lax.rem(wide_home - w + REACH + wide_size, wide_size) - REACH
    toward = offset * sign
    slot = jnp.where(toward > 0, 2 * toward - 1, -2 * toward)
    is_live = lax.broadcasted_iota(jnp.int32, (1, pairs), 1) < count[0]
    slot_own[...] = jnp.where(is_live, slot * TB_DEV + home[...] - wide_home * TB_DEV, -1)

    pl.semaphore_wait(barrier, 4)
    own_cells = tiles * cells
    entry = [
        remote(
            field.at[:, :, pl.ds(pl.multiple_of(other * own_cells, own_cells), own_cells)],
            field_in,
            entry_sems,
            (0,),
            (w, other),
        ),
        remote(slot_own, slot_in, entry_sems, (1,), (w, other)),
    ]
    for copy in entry:
        copy.start()

    level_ids = lax.broadcasted_iota(jnp.int32, (levels, cells), 0)

    def stack(side, group, read):
        for tile in range(tiles):
            wet = level_ids + group * levels < depth[pl.ds(tile, 1), :]
            for k in range(components):
                value = read(k, tile).astype(jnp.float32) if k < fields else 1.0
                stacked[tile, pl.ds(side * rows + k * levels, levels), :] = jnp.where(
                    wet, value, 0.0
                )

    small[3].wait()
    small[4].wait()
    own_start = n * own_cells
    stack(
        1,
        n,
        lambda k, tile: field[k, :, pl.ds(pl.multiple_of(own_start + tile * cells, cells), cells)],
    )

    half = cells // 2
    for i in range(LOADS):
        loads[i].wait()

        def unpack(step, carry):
            for u in range(UNROLL):
                p = i * per_load + step * UNROLL + u
                word = words[p]
                low = (word & 65535).astype(jnp.float32).astype(jnp.bfloat16)
                high = (word >> 16).astype(jnp.float32).astype(jnp.bfloat16)
                weight[p, pl.ds(0, half), :] = low
                weight[p, pl.ds(half, half), :] = high
            return carry

        lax.fori_loop(0, per_load // UNROLL, unpack, 0)

    entry[0].wait()
    stack(0, other, lambda k, tile: field_in[k, :, pl.ds(tile * cells, cells)])

    per_batch = pairs // BATCHES

    def rounded(side, level, k, start, count):
        row = side * rows + k * levels + level
        return terms[pl.ds(row * pairs + start, count), :].astype(jnp.bfloat16)

    cross = []
    for batch in range(BATCHES):
        first = batch * per_batch

        def multiply(step, carry):
            for u in range(UNROLL):
                p = first + step * UNROLL + u
                values = stacked[source[p]].astype(jnp.bfloat16)
                term = lax.dot_general(
                    values, weight[p], (((1,), (1,)), ((), ())),
                    preferred_element_type=jnp.float32,
                )
                terms[pl.ds(p, 2 * rows, stride=pairs), :] = term * (1.0 / DENOM)
            return carry

        lax.fori_loop(0, per_batch // UNROLL, multiply, 0)
        span = pl.ds(first, per_batch)
        for level in range(EARLY):
            for k in range(components):
                cross_out[level, k, span, :] = rounded(0, level, k, first, per_batch)
            copy = remote(
                cross_out.at[level, :, span, :],
                cross_in.at[level, :, span, :],
                early_sems,
                (level, batch),
                (w, other),
            )
            copy.start()
            cross.append((level, copy))
    for level in range(EARLY, levels):
        for k in range(components):
            cross_out[level, k] = rounded(0, level, k, 0, pairs)
        copy = remote(
            cross_out.at[level], cross_in.at[level], cross_sems, (level - EARLY,), (w, other)
        )
        copy.start()
        cross.append((level, copy))
    for level in range(levels):
        for k in range(components):
            own_terms[level, k] = rounded(1, level, k, 0, pairs)

    entry[1].wait()
    slots = lax.broadcasted_iota(jnp.int32, (5 * TB_DEV, pairs), 0)
    select = jnp.concatenate(
        [
            jnp.where(slots == slot_own[...], 1.0, 0.0).astype(jnp.bfloat16),
            jnp.where(slots == slot_in[...], 1.0, 0.0).astype(jnp.bfloat16),
        ],
        axis=1,
    )

    to_mate, to_ahead, to_behind = [], [], []

    def pass_on(level):
        to_mate[level].wait_recv()
        for k in range(components):
            sums_out[level, AHEAD - 1, k] = (
                sums_out[level, AHEAD - 1, k].astype(jnp.float32)
                + mate_in[level, RELAY - 1, k].astype(jnp.float32)
            ).astype(jnp.bfloat16)
        copy = remote(
            sums_out.at[level, AHEAD - 1], ahead_in.at[level], ahead_sems, (level,), (ahead, n)
        )
        copy.start()
        to_ahead.append(copy)

    for level in range(levels):
        for of_level, copy in cross:
            if of_level == level:
                copy.wait_recv()
        for k in range(components):
            pair_values = jnp.concatenate([own_terms[level, k], cross_in[level, k]], axis=0)
            sums = jnp.dot(select, pair_values, preferred_element_type=jnp.float32)
            self_sum[level, k] = sums[:TB_DEV]
            for slot in (MATE, RELAY, AHEAD, BEHIND):
                sums_out[level, slot - 1, k] = sums[
                    slot * TB_DEV : (slot + 1) * TB_DEV
                ].astype(jnp.bfloat16)
        copy = remote(
            sums_out.at[level, pl.ds(0, 2)], mate_in.at[level], mate_sems, (level,), (mate, n)
        )
        copy.start()
        to_mate.append(copy)
        copy = remote(
            sums_out.at[level, BEHIND - 1], behind_in.at[level], behind_sems, (level,), (behind, n)
        )
        copy.start()
        to_behind.append(copy)
        if level > 0:
            pass_on(level - 1)
    pass_on(levels - 1)

    for level in range(levels):
        to_behind[level].wait_recv()
        to_ahead[level].wait_recv()

        def total(k):
            return (
                self_sum[level, k]
                + mate_in[level, MATE - 1, k].astype(jnp.float32)
                + ahead_in[level, k].astype(jnp.float32)
                + behind_in[level, k].astype(jnp.float32)
            )

        wet_total = total(fields)
        covered = wet_total > wet_limit
        safe_wet = jnp.where(covered, wet_total, 1.0)
        for k in range(fields):
            out_ref[k, level] = jnp.where(covered, total(k) / safe_wet, 0.0).astype(out_ref.dtype)
    for _, copy in cross:
        copy.wait_send()
    for copy in to_mate + to_ahead + to_behind:
        copy.wait_send()


def by_kernel(src_field, src_depth, packed_counts, pair_source, pair_home, pair_count):
    wide_size = lax.axis_size("wide")
    fields, levels, _ = src_field.shape
    pairs, _, cells = packed_counts.shape
    tiles = src_depth.shape[0] // cells
    components = fields + 1
    rows = components * levels
    sizes = (wide_size, fields, levels, tiles, cells, pairs)
    hbm = pl.BlockSpec(memory_space=pltpu.HBM)
    bf16, f32, i32 = jnp.bfloat16, jnp.float32, jnp.int32
    terms_shape = (levels, components, pairs, cells)
    sums_shape = (components, TB_DEV, cells)
    copies = pltpu.SemaphoreType.DMA((2, levels))
    result = pl.pallas_call(
        functools.partial(remap_kernel, sizes),
        out_shape=jax.ShapeDtypeStruct((fields, levels, TB_DEV, cells), bf16),
        in_specs=[hbm] * 6,
        out_specs=pl.BlockSpec(memory_space=pltpu.VMEM),
        scratch_shapes=[
            pltpu.VMEM(src_field.shape, bf16),
            pltpu.VMEM((tiles, cells), i32),
            pltpu.SMEM((pairs,), i32),
            pltpu.VMEM((1, pairs), i32),
            pltpu.SMEM((1,), i32),
            pltpu.VMEM((fields, levels, tiles * cells), bf16),
            pltpu.VMEM((1, pairs), i32),
            pltpu.VMEM((1, pairs), i32),
            pltpu.VMEM((pairs, cells // 2, cells), i32),
            pltpu.VMEM((pairs, cells, cells), bf16),
            pltpu.VMEM((tiles, 2 * rows, cells), f32),
            pltpu.VMEM((2 * rows * pairs, cells), f32),
            pltpu.VMEM(terms_shape, bf16),
            pltpu.VMEM(terms_shape, bf16),
            pltpu.VMEM(terms_shape, bf16),
            pltpu.VMEM((levels,) + sums_shape, f32),
            pltpu.VMEM((levels, 4) + sums_shape, bf16),
            pltpu.VMEM((levels, 2) + sums_shape, bf16),
            pltpu.VMEM((levels,) + sums_shape, bf16),
            pltpu.VMEM((levels,) + sums_shape, bf16),
            pltpu.SemaphoreType.DMA((LOADS,)),
            pltpu.SemaphoreType.DMA((5,)),
            pltpu.SemaphoreType.DMA((2, 2)),
            pltpu.SemaphoreType.DMA((2, EARLY, BATCHES)),
            pltpu.SemaphoreType.DMA((2, levels - EARLY)),
            copies,
            copies,
            copies,
        ],
        compiler_params=pltpu.CompilerParams(
            collective_id=0, has_side_effects=True, vmem_limit_bytes=67043328
        ),
        name="remap",
    )(
        src_field,
        src_depth.reshape(tiles, cells),
        packed_counts,
        pair_source,
        pair_home.reshape(1, pairs),
        pair_count,
    )
    return result.reshape(fields, levels, TB_DEV * cells)


def solution(mesh):
    placed = (
        P(None, "narrow", "wide"),
        P(("wide", "narrow")),
        P(("wide", "narrow"), None, None),
        P(("wide", "narrow")),
        P(("wide", "narrow")),
        P(("wide", "narrow")),
    )
    paired = mesh.shape["narrow"] == 2 and mesh.shape["wide"] % 2 == 0
    fits = paired and mesh.shape["wide"] > 2 * REACH and REACH == 2
    return jax.shard_map(
        by_kernel if fits else by_collectives,
        mesh=mesh,
        in_specs=placed,
        out_specs=P(None, "narrow", "wide"),
        check_vma=False,
    )
```

time: 48.2 us -> 40.6 us (0.84)
  local copies, waits for them, and re-layouts: 5.25 us -> 1.77 us
  Pallas kernels: 41.4 us -> 38 us
  other arithmetic: 0.68 us -> 0 us
    unnamed x8 -> x0, local copies, waits for them, and re-layouts: 4.44 us -> none
    pallas_call x1, Pallas kernels: 41.4 us -> 38 us  [by_kernel(): pl.pallas_call(functools.partial(remap_kernel, sizes), out_shape=jax.Shap...]
    reshape x1, local copies, waits for them, and re-layouts: 0.82 us -> 1.77 us  [by_kernel(): return result.reshape(fields, levels, TB_DEV * cells)]
    reshape x1 -> x0, other arithmetic: 0.68 us -> none  [by_kernel(): home.reshape(1, pairs)]
where the time goes in v2:
time: 40.6 us; the launch traced here: 40.4 us
  Pallas kernels  38 us (94%)
  local copies, waits for them, and re-layouts  1.77 us (4%)
  between operations  0.66 us (2%)
    pallas_call x1, Pallas kernels, by_kernel(): pl.pallas_call(functools.partial(remap_kernel, sizes), out_shape=jax.Shap...  38 us
    reshape x1, local copies, waits for them, and re-layouts, by_kernel(): return result.reshape(fields, levels, TB_DEV * cells)  1.77 us

profile of v2, /device:TPU:0, one launch (start us, length us, event | category | flops | bytes accessed | tf_op | source)
XLA Modules:
  0.0 40.4 jit_solution(7835820336683378646)
XLA Ops:
  0.7 38.0 %remap.1 = bf16[2,8,64,128]{3,2,1,0:T(8,128)(2,1)} custom-call(bf16[2,8,4096]{2,1,0:T(8,128)(2,1)} %field_hbm.1, s32[16,128]{1,0:T(8,128)} %bitcast.4, s32[128,64,128]{2,1,0:T(8,128)} %packed_hbm.1, s32[128]{0:T(128)} %source_hbm.1, s32[1,128]{1,0:T(1,128)} %bitcast.5, s32[1]{0:T(128)S(6)} %copy.7.count_hbm), custom_call_target="tpu_custom_call" | custom-call | tf_op jit(solution)/shard_map/remap/pallas_call | solution.py:395
  38.7 1.8 %reshape.11 = bf16[2,8,8192]{2,1,0:T(8,128)(2,1)} reshape(bf16[2,8,64,128]{3,2,1,0:T(8,128)(2,1)} %remap.1) | data formatting | bytes 524288 | tf_op jit(solution)/shard_map/reshape | solution.py:442

commit v3 on v2

--- a/solution.py
+++ b/solution.py
@@ -105,7 +105,8 @@
 LOADS = 8
 BATCHES = 4
 EARLY = 3
-UNROLL = 4
+UNROLL = 16
+SKEW = 8
 
 
 def remap_kernel(
@@ -149,6 +150,7 @@
     wide_size, fields, levels, tiles, cells, pairs = sizes
     components = fields + 1
     rows = components * levels
+    pitch = pairs + SKEW
     w = lax.axis_index("wide")
     n = lax.axis_index("narrow")
     other = 1 - n
@@ -262,7 +264,7 @@
 
     def rounded(side, level, k, start, count):
         row = side * rows + k * levels + level
-        return terms[pl.ds(row * pairs + start, count), :].astype(jnp.bfloat16)
+        return terms[pl.ds(row * pitch + start, count), :].astype(jnp.bfloat16)
 
     cross = []
     for batch in range(BATCHES):
@@ -276,7 +278,7 @@
                     values, weight[p], (((1,), (1,)), ((), ())),
                     preferred_element_type=jnp.float32,
                 )
-                terms[pl.ds(p, 2 * rows, stride=pairs), :] = term * (1.0 / DENOM)
+                terms[pl.ds(p, 2 * rows, stride=pitch), :] = term * (1.0 / DENOM)
             return carry
 
         lax.fori_loop(0, per_batch // UNROLL, multiply, 0)
@@ -409,7 +411,7 @@
             pltpu.VMEM((pairs, cells // 2, cells), i32),
             pltpu.VMEM((pairs, cells, cells), bf16),
             pltpu.VMEM((tiles, 2 * rows, cells), f32),
-            pltpu.VMEM((2 * rows * pairs, cells), f32),
+            pltpu.VMEM((2 * rows * (pairs + SKEW), cells), f32),
             pltpu.VMEM(terms_shape, bf16),
             pltpu.VMEM(terms_shape, bf16),
             pltpu.VMEM(terms_shape, bf16),

time: 40.6 us -> 38.9 us (0.958)
  Pallas kernels: 38 us -> 36.3 us
    pallas_call x1, Pallas kernels: 38 us -> 36.3 us  [by_kernel(): pl.pallas_call(functools.partial(remap_kernel, sizes), out_shape=jax.Shap...]
where the time goes in v3:
time: 38.9 us; the launch traced here: 38.7 us
  Pallas kernels  36.3 us (93%)
  local copies, waits for them, and re-layouts  1.77 us (5%)
  between operations  0.66 us (2%)
    pallas_call x1, Pallas kernels, by_kernel(): pl.pallas_call(functools.partial(remap_kernel, sizes), out_shape=jax.Shap...  36.3 us
    reshape x1, local copies, waits for them, and re-layouts, by_kernel(): return result.reshape(fields, levels, TB_DEV * cells)  1.77 us

profile of v3, /device:TPU:0, one launch (start us, length us, event | category | flops | bytes accessed | tf_op | source)
XLA Modules:
  0.0 38.7 jit_solution(8321167594067215667)
XLA Ops:
  0.7 36.3 %remap.1 = bf16[2,8,64,128]{3,2,1,0:T(8,128)(2,1)} custom-call(bf16[2,8,4096]{2,1,0:T(8,128)(2,1)} %field_hbm.1, s32[16,128]{1,0:T(8,128)} %bitcast.4, s32[128,64,128]{2,1,0:T(8,128)} %packed_hbm.1, s32[128]{0:T(128)} %source_hbm.1, s32[1,128]{1,0:T(1,128)} %bitcast.5, s32[1]{0:T(128)S(6)} %copy.7.count_hbm), custom_call_target="tpu_custom_call" | custom-call | tf_op jit(solution)/shard_map/remap/pallas_call | solution.py:397
  37.0 1.8 %reshape.11 = bf16[2,8,8192]{2,1,0:T(8,128)(2,1)} reshape(bf16[2,8,64,128]{3,2,1,0:T(8,128)(2,1)} %remap.1) | data formatting | bytes 524288 | tf_op jit(solution)/shard_map/reshape | solution.py:444

commit v4 on v3

--- a/solution.py
+++ b/solution.py
@@ -104,7 +104,7 @@
 SELF, MATE, RELAY, AHEAD, BEHIND = range(5)
 LOADS = 8
 BATCHES = 4
-EARLY = 3
+EARLY = 2
 UNROLL = 16
 SKEW = 8
 
@@ -196,7 +196,13 @@
             device_id_type=pl.DeviceIdType.MESH,
         )
 
+    own_cells = tiles * cells
+    theirs = pl.ds(pl.multiple_of(other * own_cells, own_cells), own_cells)
     small[0].wait()
+    pl.semaphore_wait(barrier, 4)
+    entry = [remote(field.at[:, :, theirs], field_in, entry_sems, (0,), (w, other))]
+    entry[0].start()
+
     small[1].wait()
     small[2].wait()
     wide_home = lax.div(home[...], TB_DEV)
@@ -205,21 +211,8 @@
     slot = jnp.where(toward > 0, 2 * toward - 1, -2 * toward)
     is_live = lax.broadcasted_iota(jnp.int32, (1, pairs), 1) < count[0]
     slot_own[...] = jnp.where(is_live, slot * TB_DEV + home[...] - wide_home * TB_DEV, -1)
-
-    pl.semaphore_wait(barrier, 4)
-    own_cells = tiles * cells
-    entry = [
-        remote(
-            field.at[:, :, pl.ds(pl.multiple_of(other * own_cells, own_cells), own_cells)],
-            field_in,
-            entry_sems,
-            (0,),
-            (w, other),
-        ),
-        remote(slot_own, slot_in, entry_sems, (1,), (w, other)),
-    ]
-    for copy in entry:
-        copy.start()
+    entry.append(remote(slot_own, slot_in, entry_sems, (1,), (w, other)))
+    entry[1].start()
 
     level_ids = lax.broadcasted_iota(jnp.int32, (levels, cells), 0)
 
@@ -257,31 +250,33 @@
 
         lax.fori_loop(0, per_load // UNROLL, unpack, 0)
 
-    entry[0].wait()
-    stack(0, other, lambda k, tile: field_in[k, :, pl.ds(tile * cells, cells)])
-
     per_batch = pairs // BATCHES
 
-    def rounded(side, level, k, start, count):
-        row = side * rows + k * levels + level
-        return terms[pl.ds(row * pitch + start, count), :].astype(jnp.bfloat16)
-
-    cross = []
-    for batch in range(BATCHES):
-        first = batch * per_batch
-
-        def multiply(step, carry):
+    def multiply(side, first, count):
+        def body(step, carry):
             for u in range(UNROLL):
                 p = first + step * UNROLL + u
-                values = stacked[source[p]].astype(jnp.bfloat16)
+                values = stacked[source[p], pl.ds(side * rows, rows), :].astype(jnp.bfloat16)
                 term = lax.dot_general(
                     values, weight[p], (((1,), (1,)), ((), ())),
                     preferred_element_type=jnp.float32,
                 )
-                terms[pl.ds(p, 2 * rows, stride=pitch), :] = term * (1.0 / DENOM)
+                terms[pl.ds(side * rows * pitch + p, rows, stride=pitch), :] = term * (1.0 / DENOM)
             return carry
 
-        lax.fori_loop(0, per_batch // UNROLL, multiply, 0)
+        lax.fori_loop(0, count // UNROLL, body, 0)
+
+    def rounded(side, level, k, start, count):
+        row = side * rows + k * levels + level
+        return terms[pl.ds(row * pitch + start, count), :].astype(jnp.bfloat16)
+
+    entry[0].wait()
+    stack(0, other, lambda k, tile: field_in[k, :, pl.ds(tile * cells, cells)])
+
+    cross = []
+    for batch in range(BATCHES):
+        first = batch * per_batch
+        multiply(0, first, per_batch)
         span = pl.ds(first, per_batch)
         for level in range(EARLY):
             for k in range(components):
@@ -303,6 +298,8 @@
         )
         copy.start()
         cross.append((level, copy))
+
+    multiply(1, 0, pairs)
     for level in range(levels):
         for k in range(components):
             own_terms[level, k] = rounded(1, level, k, 0, pairs)

time: 38.9 us -> 37.2 us (0.956)
  Pallas kernels: 36.3 us -> 34.7 us
    pallas_call x1, Pallas kernels: 36.3 us -> 34.7 us  [by_kernel(): pl.pallas_call(functools.partial(remap_kernel, sizes), out_shape=jax.Shap...]
where the time goes in v4:
time: 37.2 us; the launch traced here: 37.1 us
  Pallas kernels  34.7 us (93%)
  local copies, waits for them, and re-layouts  1.77 us (5%)
  between operations  0.66 us (2%)
    pallas_call x1, Pallas kernels, by_kernel(): pl.pallas_call(functools.partial(remap_kernel, sizes), out_shape=jax.Shap...  34.7 us
    reshape x1, local copies, waits for them, and re-layouts, by_kernel(): return result.reshape(fields, levels, TB_DEV * cells)  1.77 us

profile of v4, /device:TPU:0, one launch (start us, length us, event | category | flops | bytes accessed | tf_op | source)
XLA Modules:
  0.0 37.1 jit_solution(1402938981574424243)
XLA Ops:
  0.7 34.7 %remap.1 = bf16[2,8,64,128]{3,2,1,0:T(8,128)(2,1)} custom-call(bf16[2,8,4096]{2,1,0:T(8,128)(2,1)} %field_hbm.1, s32[16,128]{1,0:T(8,128)} %bitcast.4, s32[128,64,128]{2,1,0:T(8,128)} %packed_hbm.1, s32[128]{0:T(128)} %source_hbm.1, s32[1,128]{1,0:T(1,128)} %bitcast.5, s32[1]{0:T(128)S(6)} %copy.7.count_hbm), custom_call_target="tpu_custom_call" | custom-call | tf_op jit(solution)/shard_map/remap/pallas_call | solution.py:394
  35.3 1.8 %reshape.11 = bf16[2,8,8192]{2,1,0:T(8,128)(2,1)} reshape(bf16[2,8,64,128]{3,2,1,0:T(8,128)(2,1)} %remap.1) | data formatting | bytes 524288 | tf_op jit(solution)/shard_map/reshape | solution.py:441
